TPU v7x, 32 devices: a 4x4x1 block of a 4x4x8 slice. The times are simulated.
32 devices in a mesh: part: 1 (over z), data: 4 (over y), stage: 8 (over x, core).
Axes of the slice: x: 4, y: 4, z: 1, core: 2. Of those that a mesh axis runs over, the one named last changes fastest.
The devices are a block of a 4x4x8 slice.
Arguments:
- x_in: bfloat16 [8, 64, 512], P(('part', 'data'))
- y_tgt: bfloat16 [8, 64, 512], P(('part', 'data'))
- w_up: bfloat16 [32, 512, 2048], P('stage')
- w_down: bfloat16 [32, 2048, 512], P('stage')
- gain: float32 [32, 512], P('stage')
Outputs:
- output 1: float32 [32, 512, 2048], P(('part', 'stage'))
- output 2: float32 [32, 2048, 512], P(('part', 'stage'))
- output 3: float32 [32, 512], P(('part', 'stage'))
- output 4: float32 [1], P('part')
All inputs are finite; a program needn't handle non-finite values.
Results may differ from a plain program's by a relative error of at most 0.0155895.
Values are sent between devices in bfloat16 or wider.
A program may use at most 768 MiB of HBM per device.

v0:
```python
import jax
import jax.numpy as jnp
from jax import lax
from jax.sharding import PartitionSpec as P

EPS = 1e-6
ROW_DIMS = (((0,), (0,)), ((), ()))
LAST_DIMS = (((1,), (1,)), ((), ()))


def layer_fwd(x_rows, w_one, w_two, gain_row):
    x_float = x_rows.astype(jnp.float32)
    inv_rms = lax.rsqrt(jnp.mean(x_float * x_float, axis=-1, keepdims=True) + EPS)
    normed = (x_float * inv_rms * gain_row).astype(jnp.bfloat16)
    pre_act = jnp.dot(normed, w_one, preferred_element_type=jnp.float32)
    hidden = jax.nn.gelu(pre_act).astype(jnp.bfloat16)
    update = jnp.dot(hidden, w_two, preferred_element_type=jnp.float32)
    return (x_float + update).astype(jnp.bfloat16)


def layer_bwd(x_rows, d_out, w_one, w_two, gain_row):
    x_float = x_rows.astype(jnp.float32)
    inv_rms = lax.rsqrt(jnp.mean(x_float * x_float, axis=-1, keepdims=True) + EPS)
    unit_x = x_float * inv_rms
    normed = (unit_x * gain_row).astype(jnp.bfloat16)
    pre_act = jnp.dot(normed, w_one, preferred_element_type=jnp.float32)
    act_full, gelu_back = jax.vjp(jax.nn.gelu, pre_act)
    hidden = act_full.astype(jnp.bfloat16)
    g_two = lax.dot_general(hidden, d_out, ROW_DIMS, preferred_element_type=jnp.float32)
    d_hidden = lax.dot_general(d_out, w_two, LAST_DIMS, preferred_element_type=jnp.float32)
    d_pre = gelu_back(d_hidden)[0].astype(jnp.bfloat16)
    g_one = lax.dot_general(normed, d_pre, ROW_DIMS, preferred_element_type=jnp.float32)
    d_normed = lax.dot_general(d_pre, w_one, LAST_DIMS, preferred_element_type=jnp.float32)
    g_gain = jnp.sum(d_normed * unit_x, axis=0)
    d_unit = d_normed * gain_row
    d_x = inv_rms * (d_unit - unit_x * jnp.mean(d_unit * unit_x, axis=-1, keepdims=True))
    return (d_out.astype(jnp.float32) + d_x).astype(jnp.bfloat16), g_one, g_two, g_gain


def stage_fwd(x_rows, old_saved, w_one, w_two, gains):
    layer_inputs = []
    hidden_x = x_rows
    for layer_id in range(w_one.shape[0]):
        layer_inputs.append(hidden_x)
        hidden_x = layer_fwd(hidden_x, w_one[layer_id], w_two[layer_id], gains[layer_id])
    return hidden_x, jnp.stack(layer_inputs)


def keep_fwd(x_rows, old_saved, w_one, w_two, gains):
    return x_rows, old_saved


def stage_bwd(saved_x, d_out, w_one, w_two, gains, acc_all):
    list_one = []
    list_two = []
    list_gain = []
    d_rows = d_out
    for layer_id in reversed(range(w_one.shape[0])):
        d_rows, g_one, g_two, g_gain = layer_bwd(saved_x[layer_id], d_rows, w_one[layer_id], w_two[layer_id], gains[layer_id])
        list_one.append(g_one)
        list_two.append(g_two)
        list_gain.append(g_gain)
    acc_one, acc_two, acc_gain = acc_all
    return d_rows, (acc_one + jnp.stack(list_one[::-1]), acc_two + jnp.stack(list_two[::-1]), acc_gain + jnp.stack(list_gain[::-1]))


def keep_bwd(saved_x, d_out, w_one, w_two, gains, acc_all):
    return d_out, acc_all


def solution(mesh):
    n_stage = mesh.shape["stage"]
    n_data = mesh.shape["data"]
    last_stage = n_stage - 1
    east_perm = [(idx_dev, idx_dev + 1) for idx_dev in range(n_stage - 1)]
    west_perm = [(idx_dev + 1, idx_dev) for idx_dev in range(n_stage - 1)]
    mirror_perm = [(idx_dev, n_stage - 1 - idx_dev) for idx_dev in range(n_stage)]

    def local_step(x_in, y_tgt, w_up, w_down, gain):
        n_micro, tokens, width = x_in.shape
        half_micro = n_micro // 2
        depth_local, ff_width = w_up.shape[0], w_up.shape[2]
        tok_total = n_data * n_micro * tokens
        stage_id = lax.axis_index("stage")
        own_w = (w_up, w_down, gain)
        mirror_w = (lax.ppermute(w_up, "stage", mirror_perm), lax.ppermute(w_down, "stage", mirror_perm), lax.ppermute(gain, "stage", mirror_perm))
        x_east = x_in[:half_micro]
        x_west = x_in[half_micro:]
        y_east = y_tgt[:half_micro]
        y_west = y_tgt[half_micro:]

        def fwd_dir(k_micro, recv_rows, stash, top_grad, x_src, y_src, is_first, is_last, weights):
            on_mb = (k_micro >= 0) & (k_micro < half_micro)
            at_mb = jnp.clip(k_micro, 0, half_micro - 1)
            x_rows = jnp.where(is_first, lax.dynamic_index_in_dim(x_src, at_mb, 0, False), recv_rows)
            old_saved = lax.dynamic_index_in_dim(stash, at_mb, 0, False)
            out_rows, saved_new = lax.cond(on_mb, stage_fwd, keep_fwd, x_rows, old_saved, weights[0], weights[1], weights[2])
            stash = lax.dynamic_update_index_in_dim(stash, saved_new, at_mb, 0)
            err_rows = out_rows.astype(jnp.float32) - lax.dynamic_index_in_dim(y_src, at_mb, 0, False).astype(jnp.float32)
            at_end = on_mb & is_last
            top_new = jnp.where(at_end, (err_rows / tok_total).astype(jnp.bfloat16), lax.dynamic_index_in_dim(top_grad, at_mb, 0, False))
            top_grad = lax.dynamic_update_index_in_dim(top_grad, top_new, at_mb, 0)
            loss_add = jnp.where(at_end, jnp.sum(err_rows * err_rows), 0.0)
            return out_rows, stash, top_grad, loss_add

        def fwd_step(state_in, step_t):
            recv_east, recv_west, stash_east, stash_west, top_east, top_west, loss_sum = state_in
            out_east, stash_east, top_east, add_east = fwd_dir(step_t - stage_id, recv_east, stash_east, top_east, x_east, y_east, stage_id == 0, stage_id == last_stage, own_w)
            out_west, stash_west, top_west, add_west = fwd_dir(step_t - (last_stage - stage_id), recv_west, stash_west, top_west, x_west, y_west, stage_id == last_stage, stage_id == 0, mirror_w)
            recv_east = lax.ppermute(out_east, "stage", east_perm)
            recv_west = lax.ppermute(out_west, "stage", west_perm)
            return (recv_east, recv_west, stash_east, stash_west, top_east, top_west, loss_sum + add_east + add_west), None

        zero_rows = jnp.zeros((tokens, width), jnp.bfloat16)
        zero_stash = jnp.zeros((half_micro, depth_local, tokens, width), jnp.bfloat16)
        zero_top = jnp.zeros((half_micro, tokens, width), jnp.bfloat16)
        fwd_init = (zero_rows, zero_rows, zero_stash, zero_stash, zero_top, zero_top, jnp.zeros((), jnp.float32))
        n_steps = half_micro + n_stage - 1
        fwd_state = lax.scan(fwd_step, fwd_init, jnp.arange(n_steps))[0]
        stash_east, stash_west, top_east, top_west, loss_sum = fwd_state[2:]

        def bwd_dir(k_micro, recv_rows, stash, top_grad, is_last, weights, acc_all):
            on_mb = (k_micro >= 0) & (k_micro < half_micro)
            at_mb = jnp.clip(k_micro, 0, half_micro - 1)
            d_rows = jnp.where(is_last, lax.dynamic_index_in_dim(top_grad, at_mb, 0, False), recv_rows)
            saved_x = lax.dynamic_index_in_dim(stash, at_mb, 0, False)
            return lax.cond(on_mb, stage_bwd, keep_bwd, saved_x, d_rows, weights[0], weights[1], weights[2], acc_all)

        def bwd_step(state_in, step_t):
            back_east, back_west, acc_east, acc_west = state_in
            dx_east, acc_east = bwd_dir(step_t - (last_stage - stage_id), back_east, stash_east, top_east, stage_id == last_stage, own_w, acc_east)
            dx_west, acc_west = bwd_dir(step_t - stage_id, back_west, stash_west, top_west, stage_id == 0, mirror_w, acc_west)
            back_east = lax.ppermute(dx_east, "stage", west_perm)
            back_west = lax.ppermute(dx_west, "stage", east_perm)
            return (back_east, back_west, acc_east, acc_west), None

        zero_acc = (jnp.zeros((depth_local, width, ff_width), jnp.float32), jnp.zeros((depth_local, ff_width, width), jnp.float32), jnp.zeros((depth_local, width), jnp.float32))
        bwd_state = lax.scan(bwd_step, (zero_rows, zero_rows, zero_acc, zero_acc), jnp.arange(n_steps))[0]
        acc_east, acc_west = bwd_state[2], bwd_state[3]
        from_mirror = lax.ppermute(acc_west, "stage", mirror_perm)
        stage_sum = jax.tree.map(lambda own_acc, far_acc: own_acc + far_acc, acc_east, from_mirror)
        total_grads = lax.psum(stage_sum, "data")
        loss_all = lax.psum(loss_sum, ("data", "stage")) / (tok_total * width)
        return total_grads[0], total_grads[1], total_grads[2], loss_all.reshape(1)

    return jax.shard_map(local_step, mesh=mesh, in_specs=(P(("part", "data"), None, None), P(("part", "data"), None, None), P("stage", None, None), P("stage", None, None), P("stage", None)), out_specs=(P(("part", "stage"), None, None), P(("part", "stage"), None, None), P(("part", "stage"), None), P("part")), check_vma=False)
```

profile of v0, /device:TPU:97, one launch (start us, length us, event | category | flops | bytes accessed | tf_op | source)
XLA Modules:
  0.0 2561.9 jit_solution(9800339405951657170)
XLA Ops:
  7.2 4.3 collective-permute-start.5
  11.7 2.8 collective-permute-start.4
  15.5 357.3 %collective-permute-done.4 = f32[4,512]{1,0:T(4,128)S(1)} collective-permute-done((f32[4,512]{1,0:T(4,128)}, f32[4,512]{1,0:T(4,128)S(1)}, u32[]{:S(2)}, u32[]{:S(2)}) %collective-permute-start.4) | collective-permute-done | bytes 8224 | tf_op jit(solution)/shard_map/ppermute | solution.py:86
  373.6 201.8 %while.48 = (s32[]{:T(128)}, bf16[64,512]{1,0:T(8,128)(2,1)S(1)}, bf16[64,512]{1,0:T(8,128)(2,1)S(1)}, bf16[1,4,64,512]{3,2,1,0:T(8,128)(2,1)}, bf16[1,4,64,512]...) while((s32[]{:T(128)}, bf16[64,512]{1,0:T(8,128)(2,1)S(1)}, ...), condition=%wide.region_15.16_spmd, body=%wide.region_0.15_spmd.sunk | while | flops 2161115648 | bytes 38070864 | solution.py:119
  377.6 16.5 collective-permute-start.1
  398.1 14.8 conditional.8
  399.1 3.3 fusion.123
  402.3 3.3 fusion.126
  405.7 3.3 fusion.129
  408.9 3.2 fusion.36
  422.5 17.5 collective-permute-start
  447.6 2.7 collective-permute-start
  455.7 12.8 collective-permute-done.1
  469.8 2.7 collective-permute-start
  480.2 28.7 %collective-permute-start = (bf16[64,512]{1,0:T(8,128)(2,1)S(1)}, bf16[64,512]{1,0:T(8,128)(2,1)S(1)}, u32[]{:S(2)}, u32[]{:S(2)}) collective-permute-start(bf16[64,512]{1,0:T(8,128)(2,1)S(1)} %get-tuple-element.1007), channel_id=1, source_target_pairs={{0,1},{1,2},{2,3},{3,4},{4,5},{5,6},{6,7},{8,9},{9,10},{10,11},{11... | collective-permute-start | bytes 196616 | tf_op jit(solution)/shard_map/while/body/eval_jaxpr/ppermute | solution.py:110
  514.3 15.4 collective-permute-done.1
  530.9 2.7 collective-permute-start
  534.3 13.2 conditional.9
  534.5 3.3 fusion.295
  537.8 3.3 fusion.298
  541.0 3.3 fusion.301
  544.3 3.2 fusion.208
  554.5 2.7 collective-permute-start
  557.9 14.8 collective-permute-start.1
  575.5 7.9 broadcast_in_dim.66.clone
  583.4 7.8 broadcast_in_dim.65.clone
  591.2 8.3 broadcast_in_dim.66
  599.5 8.3 broadcast_in_dim.65
  607.8 626.8 %while.49 = (s32[]{:T(128)}, bf16[64,512]{1,0:T(8,128)(2,1)S(1)}, bf16[64,512]{1,0:T(8,128)(2,1)S(1)}, f32[4,512,2048]{2,1,0:T(8,128)}, f32[4,2048,512]{2,1,0:T(...) while((s32[]{:T(128)}, bf16[64,512]{1,0:T(8,128)(2,1)S(1)}, ...), condition=%wide.region_45.46_spmd, body=%wide.region_16.45_spmd.sunk | while | flops 5473382912 | bytes 639166912 | solution.py:138
  629.7 61.2 %collective-permute-start.2 = (bf16[64,512]{1,0:T(8,128)(2,1)S(1)}, bf16[64,512]{1,0:T(8,128)(2,1)S(1)}, u32[]{:S(2)}, u32[]{:S(2)}) collective-permute-start(bf16[64,512]{1,0:T(8,128)(2,1)S(1)} %get-tuple-element.1038), channel_id=1, source_target_pairs={{1,0},{2,1},{3,2},{4,3},{5,4},{6,5},{7,6},{9,8},{10,9},{11,10},{12... | collective-permute-start | bytes 196616 | tf_op jit(solution)/shard_map/while/body/eval_jaxpr/ppermute | solution.py:133
  693.0 60.6 %conditional.11 = (bf16[64,512]{1,0:T(8,128)(2,1)S(1)}, f32[4,512,2048]{2,1,0:T(8,128)}, f32[4,2048,512]{2,1,0:T(8,128)}, f32[4,512]{1,0:T(4,128)S(1)}) conditional(s32[]{:T(128)} %convert_element_type.1097, (bf16[64,512]{1,0:T(8,128)(2,1)S(1)}, f32[4,512,2048]{2,1,0:T(8,128)}, f32[4,2048,512]{2,1,0:T(8,128)}, f32[4,512]{1,0:T(4,128)S(1)}) %tuple.171, ...), branch_computations={%region_31.31_spmd, %region_32.44_spmd} | conditional | flops 2736658688 | bytes 289764512 | solution.py:127
  712.0 2.6 fusion.690
  716.9 2.6 fusion.615
  724.4 2.8 convolution_bitcast_fusion.8
  727.2 6.5 maximum_add_fusion.4
  736.1 3.4 convolution_bitcast_fusion.12
  740.6 12.9 maximum_add_fusion.3
  758.6 3.2 collective-permute-done.2
  762.9 62.4 %collective-permute-start.3 = (bf16[64,512]{1,0:T(8,128)(2,1)S(1)}, bf16[64,512]{1,0:T(8,128)(2,1)S(1)}, u32[]{:S(2)}, u32[]{:S(2)}) collective-permute-start(bf16[64,512]{1,0:T(8,128)(2,1)S(1)} %get-tuple-element.1040), channel_id=1, source_target_pairs={{0,1},{1,2},{2,3},{3,4},{4,5},{5,6},{6,7},{8,9},{9,10},{10,11},{11... | collective-permute-start | bytes 196616 | tf_op jit(solution)/shard_map/while/body/eval_jaxpr/ppermute | solution.py:134
  828.0 3.6 collective-permute-done.2
  837.8 59.7 %collective-permute-done.2 = bf16[64,512]{1,0:T(8,128)(2,1)S(1)} collective-permute-done((bf16[64,512]{1,0:T(8,128)(2,1)S(1)}, bf16[64,512]{1,0:T(8,128)(2,1)S(1)}, u32[]{:S(2)}, u32[]{:S(2)}) %collective-permute-start.2) | collective-permute-done | bytes 65568 | tf_op jit(solution)/shard_map/while/body/eval_jaxpr/ppermute | solution.py:133
  903.7 3.2 collective-permute-done.2
  908.1 121.6 %collective-permute-start.3 = (bf16[64,512]{1,0:T(8,128)(2,1)S(1)}, bf16[64,512]{1,0:T(8,128)(2,1)S(1)}, u32[]{:S(2)}, u32[]{:S(2)}) collective-permute-start(bf16[64,512]{1,0:T(8,128)(2,1)S(1)} %get-tuple-element.1040), channel_id=1, source_target_pairs={{0,1},{1,2},{2,3},{3,4},{4,5},{5,6},{6,7},{8,9},{9,10},{10,11},{11... | collective-permute-start | bytes 196616 | tf_op jit(solution)/shard_map/while/body/eval_jaxpr/ppermute | solution.py:134
  1032.2 65.2 %collective-permute-done.2 = bf16[64,512]{1,0:T(8,128)(2,1)S(1)} collective-permute-done((bf16[64,512]{1,0:T(8,128)(2,1)S(1)}, bf16[64,512]{1,0:T(8,128)(2,1)S(1)}, u32[]{:S(2)}, u32[]{:S(2)}) %collective-permute-start.2) | collective-permute-done | bytes 65568 | tf_op jit(solution)/shard_map/while/body/eval_jaxpr/ppermute | solution.py:133
  1101.1 60.4 %conditional.10 = (bf16[64,512]{1,0:T(8,128)(2,1)S(1)}, f32[4,512,2048]{2,1,0:T(8,128)}, f32[4,2048,512]{2,1,0:T(8,128)}, f32[4,512]{1,0:T(4,128)S(1)}) conditional(s32[]{:T(128)} %convert_element_type.1096, (bf16[64,512]{1,0:T(8,128)(2,1)S(1)}, f32[4,512,2048]{2,1,0:T(8,128)}, f32[4,2048,512]{2,1,0:T(8,128)}, f32[4,512]{1,0:T(4,128)S(1)}) %tuple.169, ...), branch_computations={%region_17.17_spmd, %region_18.30_spmd} | conditional | flops 2736658688 | bytes 348484352 | solution.py:127
  1107.1 2.7 fusion.466
  1112.1 2.6 fusion.397
  1130.2 2.8 convolution_bitcast_fusion
  1133.0 6.5 maximum_add_fusion.1
  1144.6 3.8 convolution_bitcast_fusion.4
  1148.4 13.1 maximum_add_fusion
  1163.4 3.6 collective-permute-done.2
  1170.8 62.8 %collective-permute-start.2 = (bf16[64,512]{1,0:T(8,128)(2,1)S(1)}, bf16[64,512]{1,0:T(8,128)(2,1)S(1)}, u32[]{:S(2)}, u32[]{:S(2)}) collective-permute-start(bf16[64,512]{1,0:T(8,128)(2,1)S(1)} %get-tuple-element.1038), channel_id=1, source_target_pairs={{1,0},{2,1},{3,2},{4,3},{5,4},{6,5},{7,6},{9,8},{10,9},{11,10},{12... | collective-permute-start | bytes 196616 | tf_op jit(solution)/shard_map/while/body/eval_jaxpr/ppermute | solution.py:133
  1234.8 2.9 collective-permute-start.8
  1237.7 361.2 %collective-permute-done.7 = f32[4,512,2048]{2,1,0:T(8,128)} collective-permute-done((f32[4,512,2048]{2,1,0:T(8,128)}, f32[4,512,2048]{2,1,0:T(8,128)}, u32[]{:S(2)}, u32[]{:S(2)}) %collective-permute-start.7) | collective-permute-done | bytes 16777248 | tf_op jit(solution)/shard_map/ppermute | solution.py:140
  1598.9 18.1 add.351
  1617.0 340.7 %collective-permute-done.8 = f32[4,2048,512]{2,1,0:T(8,128)} collective-permute-done((f32[4,2048,512]{2,1,0:T(8,128)}, f32[4,2048,512]{2,1,0:T(8,128)}, u32[]{:S(2)}, u32[]{:S(2)}) %collective-permute-start.8) | collective-permute-done | bytes 16777248 | tf_op jit(solution)/shard_map/ppermute | solution.py:140
  1957.8 12.7 add.352
  1970.7 50.4 %psum.31 = f32[]{:T(128)} all-reduce(f32[]{:T(128)} %get-tuple-element.552), channel_id=1, replica_groups=mesh['part'=1,'data'=4,'stage'=8] {'data','stage'}, use_global_device_ids=true, to_apply=%region_49.50 | all-reduce | flops 1 | bytes 8 | tf_op jit(solution)/shard_map/psum | solution.py:143
  2021.8 8.1 psum.30
  2029.9 501.1 %all-reduce.3.cloned.1.call-done = (f32[4,512,2048]{2,1,0:T(8,128)}, f32[4,2048,512]{2,1,0:T(8,128)}) async-done(((f32[4,512,2048]{2,1,0:T(8,128)}, f32[4,2048,512]{2,1,0:T(8,128)}), (f32[4,512,2048]{2,1,0:T(8,128)}, f32[4,2048,512]{2,1,0:T(8,128)})) %all-reduce.3.cloned.1.call-update) | async-done | bytes 33554448 | tf_op jit(solution)/shard_map/psum | solution.py:142
  2531.0 12.7 copy.87
  2543.7 3.7 copy-done.3
  2547.4 6.2 copy.88
  (301 shorter events, 130.0 us)
Async XLA Ops:
  7.2 2523.8 %all-reduce.3.cloned.1.call-start = ((), (), s32[]{:S(2)}) async-start(), calls=%async_computation | async-start | bytes 67108864 | tf_op jit(solution)/shard_map/psum | solution.py:142
  7.2 365.6 %collective-permute-start.5 = (bf16[4,512,2048]{2,1,0:T(8,128)(2,1)}, bf16[4,512,2048]{2,1,0:T(8,128)(2,1)}, u32[]{:S(2)}, u32[]{:S(2)}) collective-permute-start(bf16[4,512,2048]{2,1,0:T(8,128)(2,1)} %param.19), channel_id=1, source_target_pairs={{0,7},{1,6},{2,5},{3,4},{4,3},{5,2},{6,1},{7,0},{8,15},{9,14},{10,... | collective-permute-start | bytes 25165832 | tf_op jit(solution)/shard_map/ppermute | solution.py:86
  11.5 361.3 %collective-permute-start.6 = (bf16[4,2048,512]{2,1,0:T(8,128)(2,1)}, bf16[4,2048,512]{2,1,0:T(8,128)(2,1)}, u32[]{:S(2)}, u32[]{:S(2)}) collective-permute-start(bf16[4,2048,512]{2,1,0:T(8,128)(2,1)} %param.20), channel_id=1, source_target_pairs={{0,7},{1,6},{2,5},{3,4},{4,3},{5,2},{6,1},{7,0},{8,15},{9,14},{10,... | collective-permute-start | bytes 25165832 | tf_op jit(solution)/shard_map/ppermute | solution.py:86
  11.7 361.1 %collective-permute-start.4 = (f32[4,512]{1,0:T(4,128)}, f32[4,512]{1,0:T(4,128)S(1)}, u32[]{:S(2)}, u32[]{:S(2)}) collective-permute-start(f32[4,512]{1,0:T(4,128)} %param.21), channel_id=1, source_target_pairs={{0,7},{1,6},{2,5},{3,4},{4,3},{5,2},{6,1},{7,0},{8,15},{9,14},{10,... | collective-permute-start | bytes 24584 | tf_op jit(solution)/shard_map/ppermute | solution.py:86
  374.9 21.8 collective-permute-start
  377.6 19.2 collective-permute-start.1
  412.9 7.8 collective-permute-start
  415.6 5.6 collective-permute-start.1
  422.5 22.9 collective-permute-start
  440.7 5.6 collective-permute-start.1
  447.6 8.1 collective-permute-start
  451.1 17.4 collective-permute-start.1
  469.8 8.1 collective-permute-start
  473.3 5.6 collective-permute-start.1
  480.2 34.1 %collective-permute-start = (bf16[64,512]{1,0:T(8,128)(2,1)S(1)}, bf16[64,512]{1,0:T(8,128)(2,1)S(1)}, u32[]{:S(2)}, u32[]{:S(2)}) collective-permute-start(bf16[64,512]{1,0:T(8,128)(2,1)S(1)} %get-tuple-element.1007), channel_id=1, source_target_pairs={{0,1},{1,2},{2,3},{3,4},{4,5},{5,6},{6,7},{8,9},{9,10},{10,11},{11... | collective-permute-start | bytes 196616 | tf_op jit(solution)/shard_map/while/body/eval_jaxpr/ppermute | solution.py:110
  509.6 20.0 collective-permute-start.1
  530.9 21.3 collective-permute-start
  547.5 5.6 collective-permute-start.1
  554.5 21.0 collective-permute-start
  557.9 17.5 collective-permute-start.1
  599.5 8.3 copy-start.4
  627.2 63.8 %collective-permute-start.3 = (bf16[64,512]{1,0:T(8,128)(2,1)S(1)}, bf16[64,512]{1,0:T(8,128)(2,1)S(1)}, u32[]{:S(2)}, u32[]{:S(2)}) collective-permute-start(bf16[64,512]{1,0:T(8,128)(2,1)S(1)} %get-tuple-element.1040), channel_id=1, source_target_pairs={{0,1},{1,2},{2,3},{3,4},{4,5},{5,6},{6,7},{8,9},{9,10},{10,11},{11... | collective-permute-start | bytes 196616 | tf_op jit(solution)/shard_map/while/body/eval_jaxpr/ppermute | solution.py:134
  629.7 62.1 %collective-permute-start.2 = (bf16[64,512]{1,0:T(8,128)(2,1)S(1)}, bf16[64,512]{1,0:T(8,128)(2,1)S(1)}, u32[]{:S(2)}, u32[]{:S(2)}) collective-permute-start(bf16[64,512]{1,0:T(8,128)(2,1)S(1)} %get-tuple-element.1038), channel_id=1, source_target_pairs={{1,0},{2,1},{3,2},{4,3},{5,4},{6,5},{7,6},{9,8},{10,9},{11,10},{12... | collective-permute-start | bytes 196616 | tf_op jit(solution)/shard_map/while/body/eval_jaxpr/ppermute | solution.py:133
  712.0 15.2 slice-start.8
  716.9 10.3 slice-start.9
  722.1 5.1 slice-start.10
  723.6 3.6 slice-start.11
  733.7 7.0 copy-start.1
  753.6 5.0 collective-permute-start.3
  756.1 5.6 collective-permute-start.2
  762.9 65.0 %collective-permute-start.3 = (bf16[64,512]{1,0:T(8,128)(2,1)S(1)}, bf16[64,512]{1,0:T(8,128)(2,1)S(1)}, u32[]{:S(2)}, u32[]{:S(2)}) collective-permute-start(bf16[64,512]{1,0:T(8,128)(2,1)S(1)} %get-tuple-element.1040), channel_id=1, source_target_pairs={{0,1},{1,2},{2,3},{3,4},{4,5},{5,6},{6,7},{8,9},{9,10},{10,11},{11... | collective-permute-start | bytes 196616 | tf_op jit(solution)/shard_map/while/body/eval_jaxpr/ppermute | solution.py:134
  826.0 5.6 collective-permute-start.2
  832.8 5.0 collective-permute-start.3
  835.4 62.2 %collective-permute-start.2 = (bf16[64,512]{1,0:T(8,128)(2,1)S(1)}, bf16[64,512]{1,0:T(8,128)(2,1)S(1)}, u32[]{:S(2)}, u32[]{:S(2)}) collective-permute-start(bf16[64,512]{1,0:T(8,128)(2,1)S(1)} %get-tuple-element.1038), channel_id=1, source_target_pairs={{1,0},{2,1},{3,2},{4,3},{5,4},{6,5},{7,6},{9,8},{10,9},{11,10},{12... | collective-permute-start | bytes 196616 | tf_op jit(solution)/shard_map/while/body/eval_jaxpr/ppermute | solution.py:133
  898.7 5.0 collective-permute-start.3
  901.3 5.6 collective-permute-start.2
  908.1 124.1 %collective-permute-start.3 = (bf16[64,512]{1,0:T(8,128)(2,1)S(1)}, bf16[64,512]{1,0:T(8,128)(2,1)S(1)}, u32[]{:S(2)}, u32[]{:S(2)}) collective-permute-start(bf16[64,512]{1,0:T(8,128)(2,1)S(1)} %get-tuple-element.1040), channel_id=1, source_target_pairs={{0,1},{1,2},{2,3},{3,4},{4,5},{5,6},{6,7},{8,9},{9,10},{10,11},{11... | collective-permute-start | bytes 196616 | tf_op jit(solution)/shard_map/while/body/eval_jaxpr/ppermute | solution.py:134
  1030.2 67.1 %collective-permute-start.2 = (bf16[64,512]{1,0:T(8,128)(2,1)S(1)}, bf16[64,512]{1,0:T(8,128)(2,1)S(1)}, u32[]{:S(2)}, u32[]{:S(2)}) collective-permute-start(bf16[64,512]{1,0:T(8,128)(2,1)S(1)} %get-tuple-element.1038), channel_id=1, source_target_pairs={{1,0},{2,1},{3,2},{4,3},{5,4},{6,5},{7,6},{9,8},{10,9},{11,10},{12... | collective-permute-start | bytes 196616 | tf_op jit(solution)/shard_map/while/body/eval_jaxpr/ppermute | solution.py:133
  1098.6 64.8 %collective-permute-start.3 = (bf16[64,512]{1,0:T(8,128)(2,1)S(1)}, bf16[64,512]{1,0:T(8,128)(2,1)S(1)}, u32[]{:S(2)}, u32[]{:S(2)}) collective-permute-start(bf16[64,512]{1,0:T(8,128)(2,1)S(1)} %get-tuple-element.1040), channel_id=1, source_target_pairs={{0,1},{1,2},{2,3},{3,4},{4,5},{5,6},{6,7},{8,9},{9,10},{10,11},{11... | collective-permute-start | bytes 196616 | tf_op jit(solution)/shard_map/while/body/eval_jaxpr/ppermute | solution.py:134
  1101.1 9.6 copy-start.2
  1107.1 11.7 slice-start.12
  1112.1 6.7 slice-start.13
  1119.7 13.3 slice-start
  1123.9 9.0 slice-start.1
  1127.9 5.1 slice-start.2
  1129.4 3.6 slice-start.3
  1139.5 8.9 copy-start
  1161.5 5.6 collective-permute-start.2
  1168.3 65.3 %collective-permute-start.3 = (bf16[64,512]{1,0:T(8,128)(2,1)S(1)}, bf16[64,512]{1,0:T(8,128)(2,1)S(1)}, u32[]{:S(2)}, u32[]{:S(2)}) collective-permute-start(bf16[64,512]{1,0:T(8,128)(2,1)S(1)} %get-tuple-element.1040), channel_id=1, source_target_pairs={{0,1},{1,2},{2,3},{3,4},{4,5},{5,6},{6,7},{8,9},{9,10},{10,11},{11... | collective-permute-start | bytes 196616 | tf_op jit(solution)/shard_map/while/body/eval_jaxpr/ppermute | solution.py:134
  1170.8 63.6 %collective-permute-start.2 = (bf16[64,512]{1,0:T(8,128)(2,1)S(1)}, bf16[64,512]{1,0:T(8,128)(2,1)S(1)}, u32[]{:S(2)}, u32[]{:S(2)}) collective-permute-start(bf16[64,512]{1,0:T(8,128)(2,1)S(1)} %get-tuple-element.1038), channel_id=1, source_target_pairs={{1,0},{2,1},{3,2},{4,3},{5,4},{6,5},{7,6},{9,8},{10,9},{11,10},{12... | collective-permute-start | bytes 196616 | tf_op jit(solution)/shard_map/while/body/eval_jaxpr/ppermute | solution.py:133
  1234.7 364.2 %collective-permute-start.7 = (f32[4,512,2048]{2,1,0:T(8,128)}, f32[4,512,2048]{2,1,0:T(8,128)}, u32[]{:S(2)}, u32[]{:S(2)}) collective-permute-start(f32[4,512,2048]{2,1,0:T(8,128)} %get-tuple-element.547), channel_id=1, source_target_pairs={{0,7},{1,6},{2,5},{3,4},{4,3},{5,2},{6,1},{7,0},{8,15},{9,14},{10,... | collective-permute-start | bytes 50331656 | tf_op jit(solution)/shard_map/ppermute | solution.py:140
  1234.8 723.0 %collective-permute-start.8 = (f32[4,2048,512]{2,1,0:T(8,128)}, f32[4,2048,512]{2,1,0:T(8,128)}, u32[]{:S(2)}, u32[]{:S(2)}) collective-permute-start(f32[4,2048,512]{2,1,0:T(8,128)} %get-tuple-element.549), channel_id=1, source_target_pairs={{0,7},{1,6},{2,5},{3,4},{4,3},{5,2},{6,1},{7,0},{8,15},{9,14},{10,... | collective-permute-start | bytes 50331656 | tf_op jit(solution)/shard_map/ppermute | solution.py:140
  1598.9 358.9 %slice-start.4 = ((s8[16777216]{0:T(1024)(128)(4,1)}), s8[4194304]{0:T(1024)(128)(4,1)S(1)}, s32[]{:S(2)}) async-start(s8[16777216]{0:T(1024)(128)(4,1)} %bitcast.669), calls=%async_computation.5 | async-start | bytes 8388608
  1598.9 358.9 %slice-start.5 = ((s8[16777216]{0:T(1024)(128)(4,1)}), s8[4194304]{0:T(1024)(128)(4,1)S(1)}, s32[]{:S(2)}) async-start(s8[16777216]{0:T(1024)(128)(4,1)} %bitcast.669), calls=%async_computation.6 | async-start | bytes 8388608
  1598.9 358.9 %slice-start.6 = ((s8[16777216]{0:T(1024)(128)(4,1)}), s8[4194304]{0:T(1024)(128)(4,1)S(1)}, s32[]{:S(2)}) async-start(s8[16777216]{0:T(1024)(128)(4,1)} %bitcast.669), calls=%async_computation.7 | async-start | bytes 8388608
  1598.9 358.9 %slice-start.7 = ((s8[16777216]{0:T(1024)(128)(4,1)}), s8[4194304]{0:T(1024)(128)(4,1)S(1)}, s32[]{:S(2)}) async-start(s8[16777216]{0:T(1024)(128)(4,1)} %bitcast.669), calls=%async_computation.8 | async-start | bytes 8388608
  1970.6 51.2 %collective-permute-start.9 = (f32[4,512]{1,0:T(4,128)S(1)}, f32[4,512]{1,0:T(4,128)S(1)}, u32[]{:S(2)}, u32[]{:S(2)}) collective-permute-start(f32[4,512]{1,0:T(4,128)S(1)} %get-tuple-element.551), channel_id=1, source_target_pairs={{0,7},{1,6},{2,5},{3,4},{4,3},{5,2},{6,1},{7,0},{8,15},{9,14},{10,... | collective-permute-start | bytes 24584 | tf_op jit(solution)/shard_map/ppermute | solution.py:140
  2531.0 16.4 copy-start.3
Sparse Core Ops, SparseCore 0:
  1970.7 560.2 all-reduce.2
where the time goes:
time: 2570 us; the launch traced here: 2560 us
  waiting for transfers between devices  1730 us (67%)
  starting transfers between devices  448 us (17%)
  matrix products  101 us (4%)
  other arithmetic  87.5 us (3%)
  local copies, waits for them, and re-layouts  68.1 us (3%)
  blocking collectives  58.5 us (2%)
  loops' own time  50.8 us (2%)
    ppermute x3, waiting for transfers between devices, local_step(): from_mirror = lax.ppermute(acc_west, 'stage', mirror_perm)  702 us
    psum x1, waiting for transfers between devices, local_step(): total_grads = lax.psum(stage_sum, 'data')  501 us
    ppermute x1, waiting for transfers between devices, local_step(): lax.ppermute(gain, 'stage', mirror_perm)  357 us
    ppermute x8, starting transfers between devices, bwd_step(): back_west = lax.ppermute(dx_west, 'stage', east_perm)  196 us
    ppermute x8, waiting for transfers between devices, bwd_step(): back_east = lax.ppermute(dx_east, 'stage', west_perm)  140 us
    ppermute x8, starting transfers between devices, bwd_step(): back_east = lax.ppermute(dx_east, 'stage', west_perm)  137 us
    ppermute x8, starting transfers between devices, fwd_step(): recv_east = lax.ppermute(out_east, 'stage', east_perm)  61 us
  transfers between devices with their start and end apart: 39, of which 18 were waited for; matrix products, arithmetic and copies ran while one was open for 4% of the time, Pallas kernels for 0%

commit v1 on v0

v1 whole, which is shorter than its diff:
```python
import functools

import jax
import jax.numpy as jnp
from jax import lax
from jax.experimental import pallas as pl
from jax.experimental.pallas import tpu as pltpu
from jax.sharding import PartitionSpec as P

EPS = 1e-6
C1 = 0.7978845608028654
C2 = C1 * 0.044715
MESH = pl.DeviceIdType.MESH
BF = jnp.bfloat16
F32 = jnp.float32


def dot(lhs, rhs):
    return jnp.dot(lhs, rhs, preferred_element_type=F32)


def gelu_tanh(pre):
    sq = pre * pre
    return sq, jnp.tanh(pre * (C1 + C2 * sq))


def gelu_val(pre, th):
    half = 0.5 * pre
    return (half + half * th).astype(BF)


def gelu_grad(pre, sq, th):
    return (0.5 + 0.5 * th) + (0.5 * pre) * (1.0 - th * th) * (C1 + (3.0 * C2) * sq)


def unit_rows(rows):
    x_float = rows.astype(F32)
    inv_rms = lax.rsqrt(jnp.mean(x_float * x_float, axis=-1, keepdims=True) + EPS)
    return x_float, inv_rms, x_float * inv_rms


def chain_kernel(
    n_data, n_stage, tok_total, fc,
    x_hbm, y_hbm, w1_hbm, w2_hbm, gain_ref,
    rt_hbm, ut_hbm, da_hbm, dh_hbm, dgain_ref, loss_ref,
    w1s, w2s, w1t, w2t, xs, dhs, gps, dao, dast, utst, rtst, ybuf, dgs, lossb, losst,
    w1_sem, w2_sem, x_sem, y_sem, xsend, xrecv, dsend, drecv, cs_send, cs_recv, cd_send, cd_recv,
    gsend, grecv, lsend, lrecv, ls_send, ls_recv, ut_sem, rt_sem, da_sem, dao_sem, dh_sem,
):
    rep = lax.axis_index("data")
    stage = lax.axis_index("stage")
    depth, width, ff = w1s.shape
    rows = xs.shape[2]
    n_chunk = ff // fc
    last = n_stage - 1
    is_late = stage >= n_stage - 2

    def peer(step):
        return lax.rem(rep + step, n_data)

    barrier = pltpu.get_barrier_semaphore()
    for step in range(1, n_data):
        pl.semaphore_signal(barrier, inc=1, device_id={"data": peer(step)}, device_id_type=MESH)
    pl.semaphore_signal(barrier, inc=1, device_id={"stage": lax.rem(stage + 1, n_stage)}, device_id_type=MESH)
    pl.semaphore_signal(barrier, inc=1, device_id={"stage": lax.rem(stage + last, n_stage)}, device_id_type=MESH)

    def w1_copy(l):
        return pltpu.make_async_copy(w1_hbm.at[l], w1s.at[l], w1_sem.at[l])

    def w2_copy(l):
        return pltpu.make_async_copy(w2_hbm.at[l], w2s.at[l], w2_sem.at[l])

    x_copy = pltpu.make_async_copy(x_hbm, xs.at[0, rep], x_sem)
    y_copy = pltpu.make_async_copy(y_hbm, ybuf, y_sem)

    @pl.when(stage == 0)
    def _():
        x_copy.start()

    for l in range(depth):
        w1_copy(l).start()
        w2_copy(l).start()

    @pl.when(stage == last)
    def _():
        y_copy.start()

    pl.semaphore_wait(barrier, n_data + 1)

    def gather_send(buf, slot, send, recv, l, step):
        return pltpu.make_async_remote_copy(
            src_ref=buf.at[slot, rep], dst_ref=buf.at[slot, rep],
            send_sem=send.at[l, step - 1], recv_sem=recv.at[l, rep],
            device_id={"data": peer(step)}, device_id_type=MESH)

    def gather_recv(buf, slot, send, recv, l, who):
        return pltpu.make_async_remote_copy(
            src_ref=buf.at[slot, who], dst_ref=buf.at[slot, who],
            send_sem=send.at[l, 0], recv_sem=recv.at[l, who],
            device_id={"data": peer(1)}, device_id_type=MESH)

    chain_fwd = pltpu.make_async_remote_copy(
        src_ref=xs.at[depth, rep], dst_ref=xs.at[0, rep], send_sem=cs_send, recv_sem=cs_recv,
        device_id={"stage": lax.rem(stage + 1, n_stage)}, device_id_type=MESH)
    chain_bwd = pltpu.make_async_remote_copy(
        src_ref=dhs.at[0, rep], dst_ref=dhs.at[depth, rep], send_sem=cd_send, recv_sem=cd_recv,
        device_id={"stage": lax.rem(stage + last, n_stage)}, device_id_type=MESH)
    loss_down = pltpu.make_async_remote_copy(
        src_ref=losst, dst_ref=losst, send_sem=ls_send, recv_sem=ls_recv,
        device_id={"stage": lax.rem(stage + last, n_stage)}, device_id_type=MESH)

    def transpose_weights(l, carry):
        for c in range(n_chunk):
            cols = slice(c * fc, (c + 1) * fc)
            w1t[l, cols, :] = w1s[l, :, cols].T
            w2t[l, :, cols] = w2s[l, cols, :].T
        return carry

    def fwd_layer(keep_grad, l, carry):
        @pl.when(stage == 0)
        def _():
            w1_copy(l).wait()
            w2_copy(l).wait()

        for step in range(1, n_data):
            gather_send(xs, l, xsend, xrecv, l, step).start()
        x_float, inv_rms, unit = unit_rows(xs[l, rep])
        normed = (unit * gain_ref[pl.ds(l, 1), :]).astype(BF)
        acc = x_float
        for c in range(n_chunk):
            cols = slice(c * fc, (c + 1) * fc)
            pre = dot(normed, w1s[l, :, cols])
            sq, th = gelu_tanh(pre)
            if keep_grad:
                gps[l, rep, :, cols] = gelu_grad(pre, sq, th)
            acc = acc + dot(gelu_val(pre, th), w2s[l, cols, :])
        xs[l + 1, rep] = acc.astype(BF)
        return carry

    @pl.when(stage == 0)
    def _():
        x_copy.wait()

    @pl.when(stage > 0)
    def _():
        def wait_and_transpose(l, carry):
            w1_copy(l).wait()
            w2_copy(l).wait()
            return transpose_weights(l, carry)

        lax.fori_loop(0, depth, wait_and_transpose, 0)
        chain_fwd.wait_recv()

    @pl.when(is_late)
    def _():
        lax.fori_loop(0, depth, functools.partial(fwd_layer, True), 0)

    @pl.when(jnp.logical_not(is_late))
    def _():
        lax.fori_loop(0, depth, functools.partial(fwd_layer, False), 0)

    @pl.when(stage < last)
    def _():
        chain_fwd.start()

    @pl.when(stage == last)
    def _():
        y_copy.wait()
        err = xs[depth, rep].astype(F32) - ybuf[...].astype(F32)
        dhs[depth, rep] = (err / tok_total).astype(BF)
        part = jnp.sum(err * err, axis=0, keepdims=True)
        tile = part[:, 0:128]
        for c in range(1, width // 128):
            tile = tile + part[:, c * 128:(c + 1) * 128]
        lossb[rep] = jnp.broadcast_to(tile, (8, 128))

    def ut_copy(l, who, slot):
        return pltpu.make_async_copy(utst.at[slot], ut_hbm.at[l, :, pl.ds(pl.multiple_of(who * rows, rows), rows)], ut_sem.at[slot])

    def rt_copy(l, who, slot):
        return pltpu.make_async_copy(rtst.at[slot], rt_hbm.at[l, :, pl.ds(pl.multiple_of(who * rows, rows), rows)], rt_sem.at[slot])

    def saved_block(b, carry):
        l = b // n_data
        step = lax.rem(b, n_data)
        who = peer(step)
        slot = lax.rem(b, 2)

        @pl.when(step > 0)
        def _():
            gather_recv(xs, l, xsend, xrecv, l, who).wait_recv()

        @pl.when(b >= 2)
        def _():
            ut_copy(l, who, slot).wait()
            rt_copy(l, who, slot).wait()

        _, _, unit = unit_rows(xs[l, who])
        normed = (unit * gain_ref[pl.ds(l, 1), :]).astype(BF)
        rtst[slot] = normed.T
        for c in range(n_chunk):
            cols = slice(c * fc, (c + 1) * fc)
            pre = dot(normed, w1s[l, :, cols])
            sq, th = gelu_tanh(pre)
            gps[l, who, :, cols] = gelu_grad(pre, sq, th)
            utst[slot, cols, :] = gelu_val(pre, th).T
        ut_copy(l, who, slot).start()
        rt_copy(l, who, slot).start()
        return carry

    def saved_all():
        lax.fori_loop(0, depth * n_data, saved_block, 0)
        for slot in range(2):
            ut_copy(0, 0, slot).wait()
            rt_copy(0, 0, slot).wait()

    @pl.when(stage == 0)
    def _():
        lax.fori_loop(0, depth, transpose_weights, 0)

    @pl.when(jnp.logical_not(is_late))
    def _():
        saved_all()

    def dao_copy(l):
        return pltpu.make_async_copy(dao.at[l], da_hbm.at[l, rep], dao_sem.at[l])

    def bwd_layer(i, carry):
        l = depth - 1 - i
        for step in range(1, n_data):
            gather_send(dhs, l + 1, dsend, drecv, l, step).start()
        d_out = dhs[l + 1, rep]
        _, inv_rms, unit = unit_rows(xs[l, rep])
        d_normed = None
        for c in range(n_chunk):
            cols = slice(c * fc, (c + 1) * fc)
            d_hidden = dot(d_out, w2t[l, :, cols])
            d_pre = (d_hidden * gps[l, rep, :, cols]).astype(BF)
            dao[l, :, cols] = d_pre
            part = dot(d_pre, w1t[l, cols, :])
            d_normed = part if d_normed is None else d_normed + part
        dao_copy(l).start()
        d_unit = d_normed * gain_ref[pl.ds(l, 1), :]
        d_x = inv_rms * (d_unit - unit * jnp.mean(d_unit * unit, axis=-1, keepdims=True))
        dhs[l, rep] = (d_out.astype(F32) + d_x).astype(BF)
        dgs[rep, pl.ds(l, 1), :] = jnp.sum(d_normed * unit, axis=0, keepdims=True)
        return carry

    @pl.when(stage < last)
    def _():
        chain_bwd.wait_recv()

    lax.fori_loop(0, depth, bwd_layer, 0)

    @pl.when(stage > 0)
    def _():
        chain_bwd.start()

    def dg_send(step):
        return pltpu.make_async_remote_copy(
            src_ref=dgs.at[rep], dst_ref=dgs.at[rep], send_sem=gsend.at[step - 1], recv_sem=grecv.at[rep],
            device_id={"data": peer(step)}, device_id_type=MESH)

    def dg_recv(who):
        return pltpu.make_async_remote_copy(
            src_ref=dgs.at[who], dst_ref=dgs.at[who], send_sem=gsend.at[0], recv_sem=grecv.at[who],
            device_id={"data": peer(1)}, device_id_type=MESH)

    def loss_send(step):
        return pltpu.make_async_remote_copy(
            src_ref=lossb.at[rep], dst_ref=lossb.at[rep], send_sem=lsend.at[step - 1], recv_sem=lrecv.at[rep],
            device_id={"data": peer(step)}, device_id_type=MESH)

    def loss_recv(who):
        return pltpu.make_async_remote_copy(
            src_ref=lossb.at[who], dst_ref=lossb.at[who], send_sem=lsend.at[0], recv_sem=lrecv.at[who],
            device_id={"data": peer(1)}, device_id_type=MESH)

    for step in range(1, n_data):
        dg_send(step).start()

    @pl.when(stage == last)
    def _():
        for step in range(1, n_data):
            loss_send(step).start()
        for step in range(1, n_data):
            loss_recv(peer(step)).wait_recv()
        total = lossb[0]
        for who in range(1, n_data):
            total = total + lossb[who]
        losst[...] = total
        for step in range(1, n_data):
            loss_send(step).wait_send()

    @pl.when(stage < last)
    def _():
        loss_down.wait_recv()

    @pl.when(stage > 0)
    def _():
        loss_down.start()

    @pl.when(is_late)
    def _():
        saved_all()

    def da_copy(l, who, slot):
        return pltpu.make_async_copy(dast.at[slot], da_hbm.at[l, who], da_sem.at[slot])

    def dh_copy(l):
        return pltpu.make_async_copy(dhs.at[l + 1], dh_hbm.at[l], dh_sem.at[l])

    def grad_block(b, carry):
        l = depth - 1 - b // (n_data - 1)
        step = 1 + lax.rem(b, n_data - 1)
        who = peer(step)
        slot = lax.rem(b, 2)
        gather_recv(dhs, l + 1, dsend, drecv, l, who).wait_recv()

        @pl.when(step == n_data - 1)
        def _():
            dh_copy(l).start()

        @pl.when(b >= 2)
        def _():
            da_copy(l, who, slot).wait()

        d_out = dhs[l + 1, who]
        for c in range(n_chunk):
            cols = slice(c * fc, (c + 1) * fc)
            d_hidden = dot(d_out, w2t[l, :, cols])
            dast[slot, :, cols] = (d_hidden * gps[l, who, :, cols]).astype(BF)
        da_copy(l, who, slot).start()
        return carry

    lax.fori_loop(0, depth * (n_data - 1), grad_block, 0)

    for step in range(1, n_data):
        dg_recv(peer(step)).wait_recv()
    dg_total = dgs[0]
    for who in range(1, n_data):
        dg_total = dg_total + dgs[who]
    dgain_ref[...] = dg_total
    loss_ref[...] = losst[...]

    for slot in range(2):
        da_copy(0, 0, slot).wait()
    for l in range(depth):
        dao_copy(l).wait()
        dh_copy(l).wait()
        for step in range(1, n_data):
            gather_send(xs, l, xsend, xrecv, l, step).wait_send()
            gather_send(dhs, l + 1, dsend, drecv, l, step).wait_send()
    for step in range(1, n_data):
        dg_send(step).wait_send()

    @pl.when(stage < last)
    def _():
        chain_fwd.wait_send()

    @pl.when(stage > 0)
    def _():
        chain_bwd.wait_send()
        loss_down.wait_send()


def weight_grad_kernel(count, rt_ref, ut_ref, da_ref, dh_ref, dg_ref, ls_ref, d_up_ref, d_down_ref, d_gain_ref, loss_ref):
    d_up_ref[0] = dot(rt_ref[0], da_ref[0])
    d_down_ref[0] = dot(ut_ref[0], dh_ref[0])
    d_gain_ref[...] = dg_ref[...]
    loss_ref[0] = jnp.sum(ls_ref[0:1, :]) / count


def solution(mesh):
    n_stage = mesh.shape["stage"]
    n_data = mesh.shape["data"]

    def local_step(x_in, y_tgt, w_up, w_down, gain):
        n_micro, tokens, width = x_in.shape
        rows = n_micro * tokens
        depth, _, ff = w_up.shape
        all_rows = n_data * rows
        fc = min(512, ff)
        any_spec = pl.BlockSpec(memory_space=pl.ANY)
        vmem_spec = pl.BlockSpec(memory_space=pltpu.VMEM)
        dma = pltpu.SemaphoreType.DMA
        r_t, u_t, d_pre, d_out, dg_all, loss_all = pl.pallas_call(
            functools.partial(chain_kernel, n_data, n_stage, float(all_rows), fc),
            out_shape=(
                jax.ShapeDtypeStruct((depth, width, all_rows), BF),
                jax.ShapeDtypeStruct((depth, ff, all_rows), BF),
                jax.ShapeDtypeStruct((depth, n_data, rows, ff), BF),
                jax.ShapeDtypeStruct((depth, n_data, rows, width), BF),
                jax.ShapeDtypeStruct((depth, width), F32),
                jax.ShapeDtypeStruct((8, 128), F32),
            ),
            in_specs=[any_spec, any_spec, any_spec, any_spec, vmem_spec],
            out_specs=(any_spec, any_spec, any_spec, any_spec, vmem_spec, vmem_spec),
            scratch_shapes=[
                pltpu.VMEM((depth, width, ff), BF),
                pltpu.VMEM((depth, ff, width), BF),
                pltpu.VMEM((depth, ff, width), BF),
                pltpu.VMEM((depth, width, ff), BF),
                pltpu.VMEM((depth + 1, n_data, rows, width), BF),
                pltpu.VMEM((depth + 1, n_data, rows, width), BF),
                pltpu.VMEM((depth, n_data, rows, ff), F32),
                pltpu.VMEM((depth, rows, ff), BF),
                pltpu.VMEM((2, rows, ff), BF),
                pltpu.VMEM((2, ff, rows), BF),
                pltpu.VMEM((2, width, rows), BF),
                pltpu.VMEM((rows, width), BF),
                pltpu.VMEM((n_data, depth, width), F32),
                pltpu.VMEM((n_data, 8, 128), F32),
                pltpu.VMEM((8, 128), F32),
                dma((depth,)), dma((depth,)), dma, dma,
                dma((depth, n_data - 1)), dma((depth, n_data)),
                dma((depth, n_data - 1)), dma((depth, n_data)),
                dma, dma, dma, dma,
                dma((n_data - 1,)), dma((n_data,)),
                dma((n_data - 1,)), dma((n_data,)),
                dma, dma,
                dma((2,)), dma((2,)), dma((2,)), dma((depth,)), dma((depth,)),
            ],
            compiler_params=pltpu.CompilerParams(
                collective_id=0, has_side_effects=True, vmem_limit_bytes=67043328),
            name="chain",
        )(x_in.reshape(rows, width), y_tgt.reshape(rows, width), w_up, w_down, gain)
        d_pre = d_pre.reshape(depth, all_rows, ff)
        d_out = d_out.reshape(depth, all_rows, width)
        return pl.pallas_call(
            functools.partial(weight_grad_kernel, float(all_rows * width)),
            grid=(depth, ff // fc),
            out_shape=(
                jax.ShapeDtypeStruct((depth, width, ff), F32),
                jax.ShapeDtypeStruct((depth, ff, width), F32),
                jax.ShapeDtypeStruct((depth, width), F32),
                jax.ShapeDtypeStruct((1,), F32),
            ),
            in_specs=[
                pl.BlockSpec((1, width, all_rows), lambda l, c: (l, 0, 0)),
                pl.BlockSpec((1, fc, all_rows), lambda l, c: (l, c, 0)),
                pl.BlockSpec((1, all_rows, fc), lambda l, c: (l, 0, c)),
                pl.BlockSpec((1, all_rows, width), lambda l, c: (l, 0, 0)),
                pl.BlockSpec((depth, width), lambda l, c: (0, 0)),
                pl.BlockSpec((8, 128), lambda l, c: (0, 0)),
            ],
            out_specs=(
                pl.BlockSpec((1, width, fc), lambda l, c: (l, 0, c)),
                pl.BlockSpec((1, fc, width), lambda l, c: (l, c, 0)),
                pl.BlockSpec((depth, width), lambda l, c: (0, 0)),
                pl.BlockSpec(memory_space=pltpu.SMEM),
            ),
            compiler_params=pltpu.CompilerParams(vmem_limit_bytes=48 << 20),
            name="weight_grads",
        )(r_t, u_t, d_pre, d_out, dg_all, loss_all)

    return jax.shard_map(local_step, mesh=mesh, in_specs=(P(("part", "data"), None, None), P(("part", "data"), None, None), P("stage", None, None), P("stage", None, None), P("stage", None)), out_specs=(P(("part", "stage"), None, None), P(("part", "stage"), None, None), P(("part", "stage"), None), P("part")), check_vma=False)
```

time: 2570 us -> 171 us (0.07)
  the two profiles are of different devices: /device:TPU:97 before, /device:TPU:96 now
where the time goes in v1:
time: 171 us; the launch traced here: 170 us
  Pallas kernels  165 us (96%)
  local copies, waits for them, and re-layouts  4.55 us (3%)
    pallas_call x1, Pallas kernels, local_step(): pl.pallas_call(functools.partial(chain_kernel, n_data, n_stage, float(all...  142 us
    pallas_call x1, Pallas kernels, local_step(): pl.pallas_call(functools.partial(weight_grad_kernel, float(all_rows * wid...  23.5 us
    unnamed x8, local copies, waits for them, and re-layouts  4.55 us

profile of v1, /device:TPU:96, one launch (start us, length us, event | category | flops | bytes accessed | tf_op | source)
XLA Modules:
  0.0 170.3 jit_solution(2003812306199112724)
XLA Ops:
  0.6 141.6 %chain.1 = (bf16[4,512,512]{2,1,0:T(8,128)(2,1)}, bf16[4,2048,512]{2,1,0:T(8,128)(2,1)}, bf16[4,4,128,2048]{3,2,1,0:T(8,128)(2,1)}, bf16[4,4,128,512]{3,2,1,0:T(...) custom-call(bf16[128,512]{1,0:T(8,128)(2,1)} %bitcast.6, bf16[128,512]{1,0:T(8,128)(2,1)} %bitcast.7, ...), custom_call_target="tpu_custom_call" | custom-call | tf_op jit(solution)/shard_map/chain/pallas_call | solution.py:387
  142.3 0.0 copy-start
  142.3 1.6 copy-done
  143.9 0.0 copy-start.1
  143.9 1.6 copy-done.1
  145.4 0.0 copy-start.2
  145.4 0.7 copy-done.2
  146.1 0.0 copy-start.3
  146.1 0.7 copy-done.3
  146.8 23.5 %weight_grads.1 = (f32[4,512,2048]{2,1,0:T(8,128)}, f32[4,2048,512]{2,1,0:T(8,128)}, f32[4,512]{1,0:T(4,128)}, f32[1]{0:T(128)}) custom-call(bf16[4,512,512]{2,1,0:T(8,128)(2,1)S(1)} %copy-done, bf16[4,2048,512]{2,1,0:T(8,128)(2,1)} %get-tuple-element.11.ut_ref, bf16[4,512,2048]{2,1,0:T(8,128)(2,1)} %bitcast.5, bf16[4,512,512]{2,1,0:T(8,128)(2,1)S(1)} %bitcast.4, ...), custom_call_target="tpu_custom_call" | custom-call | tf_op jit(solution)/shard_map/weight_grads/pallas_call | solution.py:430
Async XLA Ops:
  142.3 1.6 copy-start
  143.9 1.6 copy-start.1
  145.4 0.7 copy-start.2
  146.1 0.7 copy-start.3
